TPU v7x, 32 devices: a whole 2x2x4 slice. The times are simulated.
32 devices in a mesh: tm: 2 (over core), space: 16 (over z, y, x).
Axes of the slice: x: 2, y: 2, z: 4, core: 2. Of those that a mesh axis runs over, the one named last changes fastest.
Arguments:
- fine: bfloat16 [8, 64, 256, 256], P('tm', 'space'), may hold values from -6 to 6
- coarse: bfloat16 [8, 32, 128, 256], P('tm', 'space'), may hold values from -6 to 6
- w_query: bfloat16 [256, 256], replicated, may hold values from -24 to 24
- w_key: bfloat16 [256, 256], replicated, may hold values from -0.375 to 0.375
- w_value: bfloat16 [256, 256], replicated, may hold values from -0.375 to 0.375
- w_out: bfloat16 [256, 256], replicated, may hold values from -0.375 to 0.375
- conv_first: bfloat16 [3, 3, 256, 256], replicated, may hold values from -0.125 to 0.125
- conv_second: bfloat16 [3, 3, 256, 256], replicated, may hold values from -0.125 to 0.125
Outputs:
- joined: bfloat16 [8, 64, 256, 256], P('tm', 'space')
All inputs are finite; a program needn't handle non-finite values.
Results may differ from a plain program's by a relative error of at most 0.009.
Values may be sent and summed in bfloat16 or wider, within the bound.
A program may use at most 128 MiB of HBM per device.

v0:
```python
import functools

import jax
import jax.numpy as jnp
import numpy as np
from jax import lax
from jax.experimental import pallas as pl
from jax.experimental.pallas import tpu as pltpu
from jax.sharding import PartitionSpec as P

HEADS = 8
CHUNKS = 4
HALO = 1
LOG2E = 1.4426950408889634
MESH = pl.DeviceIdType.MESH


def encode(frames, width):
    half = width // 2
    inverse = np.exp(-np.log(10000.0) * 2.0 * np.arange(half) / width)
    angles = np.arange(frames)[:, None] * inverse[None, :]
    return np.concatenate([np.sin(angles), np.cos(angles)], axis=1).astype(np.float32)


def lift_matrix(small):
    out = np.arange(2 * small)[:, None]
    source = np.arange(small)[None, :]
    near = out // 2
    far = np.clip(np.where(out % 2 == 0, near - 1, near + 1), 0, small - 1)
    base = 0.75 * (source == near) + 0.25 * (source == far)
    return np.concatenate([0.75 * base, 0.25 * base], axis=1).astype(jnp.bfloat16)


def attention(mine, others, pos, wq_ref, wk_ref, wv_ref, wo_ref):
    own, (tile, width) = len(mine), mine[0].shape
    depth = width // HEADS
    scale = LOG2E / (float(depth) ** 0.5)
    normed = []
    for x, place in zip(mine + others, pos):
        hidden = x.astype(jnp.float32) + place
        center = hidden - jnp.mean(hidden, axis=-1, keepdims=True)
        spread = jnp.mean(center * center, axis=-1, keepdims=True)
        normed.append((center * lax.rsqrt(spread + 1e-05)).astype(jnp.bfloat16))
    flat = jnp.concatenate(normed, axis=0)
    query = jnp.dot(flat[: own * tile], wq_ref[...], preferred_element_type=jnp.float32)
    query = query.astype(jnp.bfloat16).reshape(own, tile, width)
    key = jnp.dot(flat, wk_ref[...], preferred_element_type=jnp.float32).astype(jnp.bfloat16)
    value = jnp.dot(flat, wv_ref[...], preferred_element_type=jnp.float32).astype(jnp.bfloat16)
    rows = lax.broadcasted_iota(jnp.int32, (width, width), 0) // depth
    cols = lax.broadcasted_iota(jnp.int32, (width, width), 1) // depth
    blocks = jnp.where(rows == cols, 1.0, 0.0).astype(jnp.bfloat16)
    scores = []
    for at in range(len(normed)):
        product = query * key[at * tile : (at + 1) * tile][None]
        scores.append(jnp.dot(product.reshape(own * tile, width), blocks, preferred_element_type=jnp.float32))
    largest = functools.reduce(jnp.maximum, scores)
    total, summed = None, None
    for at, score in enumerate(scores):
        power = jnp.exp2((score - largest) * scale).reshape(own, tile, width)
        term = power * value[at * tile : (at + 1) * tile].astype(jnp.float32)[None]
        total = power if total is None else total + power
        summed = term if summed is None else summed + term
    attended = (summed / total).astype(jnp.bfloat16).reshape(own * tile, width)
    branch = jnp.dot(attended, wo_ref[...], preferred_element_type=jnp.float32)
    return branch.reshape(own, tile, width)


def spread_columns(ref, at, row, cols):
    column = lax.broadcasted_iota(jnp.int32, row.shape, 0)
    left = jnp.where(column == 0, 0.0, pltpu.roll(row, 1, 0))
    right = jnp.where(column == cols - 1, 0.0, pltpu.roll(row, cols - 1, 0))
    width = row.shape[1]
    ref[at * cols : (at + 1) * cols, :width] = left.astype(jnp.bfloat16)
    ref[at * cols : (at + 1) * cols, width : 2 * width] = row.astype(jnp.bfloat16)
    ref[at * cols : (at + 1) * cols, 2 * width :] = right.astype(jnp.bfloat16)


def conv_rows(ref, start, first, last, cols, weight_ref):
    pieces = [ref[(start + step) * cols : (start + step + 1) * cols, :] for step in range(first, last)]
    depth = ref.shape[1]
    return jnp.dot(
        jnp.concatenate(pieces, axis=1), weight_ref[first * depth : last * depth, :], preferred_element_type=jnp.float32
    )


def kernel(
    bands, halves, fine_ref, coarse_ref, pos_ref, wq_ref, wk_ref, wv_ref, wo_ref, w1_hbm, w2_hbm, lift_ref, out_ref,
    mine, other, moved, coarse, x_ref, f_ref, w1_ref, w2_ref, edges, part_out, part_in,
    local_sems, fine_send, fine_recv, halo_send, halo_recv, part_send, part_recv, out_sems,
):
    own, rows, cols, width = mine.shape
    half = rows // 2
    span = cols // CHUNKS
    early = own // 2
    place, core = lax.axis_index("space"), lax.axis_index("tm")
    has_before, has_after = place > 0, place < bands - 1

    def fine_copy(shift, chunk):
        span_at = pl.ds(pl.multiple_of(chunk * span, span), span)
        return pltpu.make_async_remote_copy(
            src_ref=fine_ref.at[:, :, span_at],
            dst_ref=other.at[pl.ds((shift - 1) * own, own), :, span_at],
            send_sem=fine_send.at[shift - 1, chunk],
            recv_sem=fine_recv.at[shift - 1, chunk],
            device_id={"tm": lax.rem(core + halves - shift, halves)},
            device_id_type=MESH,
        )

    def mine_copy(chunk):
        span_at = pl.ds(pl.multiple_of(chunk * span, span), span)
        return pltpu.make_async_copy(fine_ref.at[:, :, span_at], mine.at[:, :, span_at], local_sems.at[chunk])

    def to_after(src, dst, send, recv):
        return pltpu.make_async_remote_copy(
            src_ref=src, dst_ref=dst, send_sem=send, recv_sem=recv, device_id={"space": place + 1}, device_id_type=MESH
        )

    def to_before(src, dst, send, recv):
        return pltpu.make_async_remote_copy(
            src_ref=src, dst_ref=dst, send_sem=send, recv_sem=recv, device_id={"space": place - 1}, device_id_type=MESH
        )

    def part_up(frame):
        return to_after(part_out.at[0, frame], part_in.at[0, frame], part_send.at[0, frame], part_recv.at[0, frame])

    def part_down(frame):
        return to_before(part_out.at[1, frame], part_in.at[1, frame], part_send.at[1, frame], part_recv.at[1, frame])

    def halo_up(frames, span_at, piece):
        return to_after(
            moved.at[frames, rows : rows + HALO, span_at], moved.at[frames, 0:HALO, span_at],
            halo_send.at[0, piece], halo_recv.at[0, piece],
        )

    def halo_down(frames, span_at, piece):
        return to_before(
            moved.at[frames, HALO : 2 * HALO, span_at], moved.at[frames, rows + HALO : rows + 2 * HALO, span_at],
            halo_send.at[1, piece], halo_recv.at[1, piece],
        )

    def both(frames, span_at, piece, act_up, act_down):
        pl.when(has_after)(lambda: act_up(halo_up(frames, span_at, piece)))
        pl.when(has_before)(lambda: act_down(halo_down(frames, span_at, piece)))

    def start(copy):
        copy.start()

    def wait_send(copy):
        copy.wait_send()

    def wait_recv(copy):
        copy.wait_recv()

    def landed(frames, span_at, piece):
        pl.when(has_before)(lambda: halo_up(frames, span_at, piece).wait_recv())
        pl.when(has_after)(lambda: halo_down(frames, span_at, piece).wait_recv())

    for chunk in range(CHUNKS):
        mine_copy(chunk).start()
    own_coarse = pltpu.make_async_copy(coarse_ref, coarse, local_sems.at[CHUNKS])
    first_weights = pltpu.make_async_copy(w1_hbm, w1_ref, local_sems.at[CHUNKS + 1])
    second_weights = pltpu.make_async_copy(w2_hbm, w2_ref, local_sems.at[CHUNKS + 2])

    barrier = pltpu.get_barrier_semaphore()
    for shift in range(1, halves):
        pl.semaphore_signal(barrier, inc=1, device_id={"tm": lax.rem(core + shift, halves)}, device_id_type=MESH)

    @pl.when(has_before)
    def _():
        pl.semaphore_signal(barrier, inc=1, device_id={"space": place - 1}, device_id_type=MESH)

    @pl.when(has_after)
    def _():
        pl.semaphore_signal(barrier, inc=1, device_id={"space": place + 1}, device_id_type=MESH)

    peers = halves - 1 + has_before.astype(jnp.int32) + has_after.astype(jnp.int32)
    pl.semaphore_wait(barrier, peers)

    for shift in range(1, halves):
        for chunk in range(CHUNKS):
            fine_copy(shift, chunk).start()
    own_coarse.start()
    first_weights.start()
    second_weights.start()

    @pl.when(jnp.logical_not(has_before))
    def _():
        moved[:, 0:HALO] = jnp.zeros((own, HALO, cols, width), jnp.bfloat16)
        part_in[0] = jnp.zeros((own, cols, width), jnp.bfloat16)

    @pl.when(jnp.logical_not(has_after))
    def _():
        moved[:, rows + HALO :] = jnp.zeros((own, HALO, cols, width), jnp.bfloat16)
        part_in[1] = jnp.zeros((own, cols, width), jnp.bfloat16)

    pos = []
    for shift in range(halves):
        for frame in range(own):
            pos.append(pos_ref[pl.ds(lax.rem(core + shift, halves) * own + frame, 1), :])

    def motion_tile(chunk, row):
        span_at = pl.ds(pl.multiple_of(chunk * span, span), span)
        here = [mine[frame, row, span_at, :] for frame in range(own)]
        there = [other[frame, row, span_at, :] for frame in range(own * (halves - 1))]
        branch = attention(here, there, pos, wq_ref, wk_ref, wv_ref, wo_ref)
        for frame in range(own):
            moved[frame, row + HALO, span_at, :] = (here[frame].astype(jnp.float32) + branch[frame]).astype(jnp.bfloat16)

    def edge_step(step, carry):
        chunk, edge = step // 2, lax.rem(step, 2)
        span_at = pl.ds(pl.multiple_of(chunk * span, span), span)

        @pl.when(edge == 0)
        def _():
            mine_copy(chunk).wait()
            for shift in range(1, halves):
                fine_copy(shift, chunk).wait_recv()

        motion_tile(chunk, edge * (rows - 1))

        @pl.when((edge == 1) & (chunk == 0))
        def _():
            both(pl.ds(0, own), pl.ds(0, span), 0, start, start)

        @pl.when((edge == 1) & (chunk > 0))
        def _():
            both(pl.ds(0, early), span_at, chunk, start, start)

        return carry

    def inner_step(step, carry):
        motion_tile(step // (rows - 2), 1 + lax.rem(step, rows - 2))
        return carry

    lax.fori_loop(0, CHUNKS * 2, edge_step, 0)
    rest = pl.ds(span, cols - span)
    for frame in range(early, own):
        both(pl.ds(frame, 1), rest, CHUNKS + frame - early, start, start)
    lax.fori_loop(0, CHUNKS * (rows - 2), inner_step, 0)

    own_coarse.wait()
    first_weights.wait()
    second_weights.wait()

    def inner_copy(frame):
        return pltpu.make_async_copy(
            mine.at[frame, 1 : rows - 1], out_ref.at[frame, 1 : rows - 1], out_sems.at[0, frame]
        )

    def edge_copy(frame, side):
        row = side * (rows - 1)
        return pltpu.make_async_copy(mine.at[frame, row], out_ref.at[frame, row], out_sems.at[1 + side, frame])

    def lifted(near, far):
        return jnp.dot(lift_ref[...], jnp.concatenate([near, far], axis=0), preferred_element_type=jnp.float32)

    def conv_step(frame, carry):
        @pl.when(frame == 0)
        def _():
            landed(pl.ds(0, own), pl.ds(0, span), 0)
            for chunk in range(1, CHUNKS):
                landed(pl.ds(0, early), pl.ds(chunk * span, span), chunk)

        @pl.when(frame >= early)
        def _():
            landed(pl.ds(frame, 1), rest, CHUNKS + frame - early)

        for r in range(rows + 2 * HALO):
            spread_columns(x_ref, r, jnp.maximum(moved[frame, r].astype(jnp.float32), 0.0), cols)
        for r in range(rows):
            first = conv_rows(x_ref, r, 0, 3, cols, w1_ref)
            first = jnp.maximum(first, 0.0).astype(jnp.bfloat16).astype(jnp.float32)
            spread_columns(f_ref, r, first, cols)
        top, bottom = coarse[frame, 0], coarse[frame, half - 1]
        none = jnp.zeros_like(top)
        part = conv_rows(f_ref, rows - 1, 0, 1, cols, w2_ref) + lifted(none, bottom)
        part_out[0, frame] = part.astype(jnp.bfloat16)
        part = conv_rows(f_ref, -2, 2, 3, cols, w2_ref) + lifted(none, top)
        part_out[1, frame] = part.astype(jnp.bfloat16)
        pl.when(has_after)(lambda: part_up(frame).start())
        pl.when(has_before)(lambda: part_down(frame).start())
        for r in range(rows):
            near = coarse[frame, r // 2]
            if r == 0:
                far = jnp.where(has_before, none, near)
            elif r == rows - 1:
                far = jnp.where(has_after, none, near)
            else:
                far = coarse[frame, r // 2 - 1] if r % 2 == 0 else coarse[frame, r // 2 + 1]
            second = conv_rows(f_ref, r - 1, 1 if r == 0 else 0, 2 if r == rows - 1 else 3, cols, w2_ref)
            joined = lifted(near, far) + moved[frame, r + HALO].astype(jnp.float32) + second
            if r == 0:
                edges[frame, 0] = joined
            elif r == rows - 1:
                edges[frame, 1] = joined
            else:
                mine[frame, r] = joined.astype(jnp.bfloat16)
        inner_copy(frame).start()
        return carry

    lax.fori_loop(0, own, conv_step, 0)

    def join_step(frame, carry):
        pl.when(has_before)(lambda: part_up(frame).wait_recv())
        mine[frame, 0] = (edges[frame, 0] + part_in[0, frame].astype(jnp.float32)).astype(jnp.bfloat16)
        edge_copy(frame, 0).start()
        pl.when(has_after)(lambda: part_down(frame).wait_recv())
        mine[frame, rows - 1] = (edges[frame, 1] + part_in[1, frame].astype(jnp.float32)).astype(jnp.bfloat16)
        edge_copy(frame, 1).start()
        return carry

    lax.fori_loop(0, own, join_step, 0)
    for frame in range(own):
        inner_copy(frame).wait()
        edge_copy(frame, 0).wait()
        edge_copy(frame, 1).wait()
        pl.when(has_after)(lambda: part_up(frame).wait_send())
        pl.when(has_before)(lambda: part_down(frame).wait_send())
    for shift in range(1, halves):
        for chunk in range(CHUNKS):
            fine_copy(shift, chunk).wait_send()
    both(pl.ds(0, own), pl.ds(0, span), 0, wait_send, wait_send)
    for chunk in range(1, CHUNKS):
        both(pl.ds(0, early), pl.ds(chunk * span, span), chunk, wait_send, wait_send)
    for frame in range(early, own):
        both(pl.ds(frame, 1), rest, CHUNKS + frame - early, wait_send, wait_send)


def local(fine, coarse, w_query, w_key, w_value, w_out, conv_first, conv_second):
    own, rows, cols, width = fine.shape
    _, half, small, _ = coarse.shape
    bands, halves = lax.axis_size("space"), lax.axis_size("tm")
    pieces = CHUNKS + own - own // 2
    far = own * (halves - 1)
    any_space = pl.BlockSpec(memory_space=pl.ANY)
    vmem = pl.BlockSpec(memory_space=pltpu.VMEM)
    bf16 = jnp.bfloat16
    return pl.pallas_call(
        functools.partial(kernel, bands, halves),
        in_specs=[any_space] * 2 + [vmem] * 5 + [any_space] * 2 + [vmem],
        out_specs=any_space,
        out_shape=jax.ShapeDtypeStruct(fine.shape, bf16),
        scratch_shapes=[
            pltpu.VMEM((own, rows, cols, width), bf16),
            pltpu.VMEM((far, rows, cols, width), bf16),
            pltpu.VMEM((own, rows + 2 * HALO, cols, width), bf16),
            pltpu.VMEM((own, half, small, width), bf16),
            pltpu.VMEM(((rows + 2 * HALO) * cols, 3 * width), bf16),
            pltpu.VMEM((rows * cols, 3 * width), bf16),
            pltpu.VMEM((9 * width, width), bf16),
            pltpu.VMEM((9 * width, width), bf16),
            pltpu.VMEM((own, 2, cols, width), jnp.float32),
            pltpu.VMEM((2, own, cols, width), bf16),
            pltpu.VMEM((2, own, cols, width), bf16),
            pltpu.SemaphoreType.DMA((CHUNKS + 3,)),
            pltpu.SemaphoreType.DMA((halves - 1, CHUNKS)),
            pltpu.SemaphoreType.DMA((halves - 1, CHUNKS)),
            pltpu.SemaphoreType.DMA((2, pieces)),
            pltpu.SemaphoreType.DMA((2, pieces)),
            pltpu.SemaphoreType.DMA((2, own)),
            pltpu.SemaphoreType.DMA((2, own)),
            pltpu.SemaphoreType.DMA((3, own)),
        ],
        compiler_params=pltpu.CompilerParams(
            collective_id=0, has_side_effects=True, vmem_limit_bytes=62 * 1024 * 1024
        ),
        name="fused",
    )(
        fine, coarse, jnp.asarray(encode(own * halves, width)), w_query, w_key, w_value, w_out,
        conv_first.reshape(9 * width, width), conv_second.reshape(9 * width, width), jnp.asarray(lift_matrix(small)),
    )


def solution(mesh):
    return jax.shard_map(
        local,
        mesh=mesh,
        in_specs=(
            P("tm", "space", None, None),
            P("tm", "space", None, None),
            P(),
            P(),
            P(),
            P(),
            P(),
            P(),
        ),
        out_specs=P("tm", "space", None, None),
        check_vma=False,
    )
```

profile of v0, /device:TPU:0, one launch (start us, length us, event | category | flops | bytes accessed | tf_op | source)
XLA Modules:
  0.0 60.3 jit_solution(18049216909069987143)
XLA Ops:
  0.0 57.2 %fused.1 = bf16[4,4,256,256]{3,2,1,0:T(8,128)(2,1)} custom-call(bf16[4,4,256,256]{3,2,1,0:T(8,128)(2,1)} %fine_ref.1, bf16[4,2,128,256]{3,2,1,0:T(8,128)(2,1)} %coarse_ref.1, f32[8,256]{1,0:T(8,128)} %constant.4.clone.pos_ref, bf16[256,256]{1,0:T(8,128)(2,1)} %wq_ref.1, bf16[256,256]{1,0:T(8,128)(2,1)} %wk_ref.1, bf16[256,256]{1,0:T(8,128)(2,1)} %wv_ref.1, ...), custom_call_target="tpu_custom_call" | custom-call | tf_op jit(solution)/shard_map/fused/pallas_call | solution.py:338
  57.2 3.1 %copy.12 = bf16[4,4,256,256]{3,2,1,0:T(8,128)(2,1)} copy(bf16[4,4,256,256]{3,2,1,0:T(8,128)(2,1)} %fused.1) | data formatting | bytes 4194304
where the time goes:
time: 60.5 us; the launch traced here: 60.3 us
  Pallas kernels  57.2 us (95%)
  local copies, waits for them, and re-layouts  3.1 us (5%)
    pallas_call x1, Pallas kernels, local(): pl.pallas_call(functools.partial(kernel, bands, halves), in_specs=[any_sp...  57.2 us
    unnamed x1, local copies, waits for them, and re-layouts  3.1 us

commit v1 on v0

v1 whole, which is shorter than its diff:
```python
import functools

import jax
import jax.numpy as jnp
import numpy as np
from jax import lax
from jax.experimental import pallas as pl
from jax.experimental.pallas import tpu as pltpu
from jax.sharding import PartitionSpec as P

HEADS = 8
CHUNKS = 4
STEPS = 8
HALO = 1
LOG2E = 1.4426950408889634
MESH = pl.DeviceIdType.MESH


def encode(frames, width):
    half = width // 2
    inverse = np.exp(-np.log(10000.0) * 2.0 * np.arange(half) / width)
    angles = np.arange(frames)[:, None] * inverse[None, :]
    return np.concatenate([np.sin(angles), np.cos(angles)], axis=1).astype(np.float32)


def lift_matrix(small):
    out = np.arange(2 * small)[:, None]
    source = np.arange(small)[None, :]
    near = out // 2
    far = np.clip(np.where(out % 2 == 0, near - 1, near + 1), 0, small - 1)
    base = 0.75 * (source == near) + 0.25 * (source == far)
    return np.concatenate([0.75 * base, 0.25 * base], axis=1).astype(jnp.bfloat16)


def attention(mine, others, pos, wq_ref, wk_ref, wv_ref, wo_ref):
    own, (tile, width) = len(mine), mine[0].shape
    depth = width // HEADS
    scale = LOG2E / (float(depth) ** 0.5)
    normed = []
    for x, place in zip(mine + others, pos):
        hidden = x.astype(jnp.float32) + place
        center = hidden - jnp.mean(hidden, axis=-1, keepdims=True)
        spread = jnp.mean(center * center, axis=-1, keepdims=True)
        normed.append((center * lax.rsqrt(spread + 1e-05)).astype(jnp.bfloat16))
    flat = jnp.concatenate(normed, axis=0)
    query = jnp.dot(flat[: own * tile], wq_ref[...], preferred_element_type=jnp.float32)
    query = (query * scale).astype(jnp.bfloat16).reshape(own, tile, width)
    key = jnp.dot(flat, wk_ref[...], preferred_element_type=jnp.float32).astype(jnp.bfloat16)
    value = jnp.dot(flat, wv_ref[...], preferred_element_type=jnp.float32).astype(jnp.bfloat16)
    rows = lax.broadcasted_iota(jnp.int32, (width, width), 0) // depth
    cols = lax.broadcasted_iota(jnp.int32, (width, width), 1) // depth
    blocks = jnp.where(rows == cols, 1.0, 0.0).astype(jnp.bfloat16)
    scores = []
    for at in range(len(normed)):
        product = query * key[at * tile : (at + 1) * tile][None]
        scores.append(jnp.dot(product.reshape(own * tile, width), blocks, preferred_element_type=jnp.float32))
    largest = functools.reduce(jnp.maximum, scores)
    total, summed = None, None
    for at, score in enumerate(scores):
        power = jnp.exp2(score - largest).reshape(own, tile, width)
        term = power * value[at * tile : (at + 1) * tile].astype(jnp.float32)[None]
        total = power if total is None else total + power
        summed = term if summed is None else summed + term
    attended = (summed / total).astype(jnp.bfloat16).reshape(own * tile, width)
    branch = jnp.dot(attended, wo_ref[...], preferred_element_type=jnp.float32)
    return branch.reshape(own, tile, width)


def spread_columns(ref, at, row, cols):
    column = lax.broadcasted_iota(jnp.int32, row.shape, 0)
    left = jnp.where(column == 0, 0.0, pltpu.roll(row, 1, 0))
    right = jnp.where(column == cols - 1, 0.0, pltpu.roll(row, cols - 1, 0))
    width = row.shape[1]
    ref[at * cols : (at + 1) * cols, :width] = left.astype(jnp.bfloat16)
    ref[at * cols : (at + 1) * cols, width : 2 * width] = row.astype(jnp.bfloat16)
    ref[at * cols : (at + 1) * cols, 2 * width :] = right.astype(jnp.bfloat16)


def conv_rows(ref, start, first, last, cols, weight_ref):
    pieces = [ref[(start + step) * cols : (start + step + 1) * cols, :] for step in range(first, last)]
    depth = ref.shape[1]
    return jnp.dot(
        jnp.concatenate(pieces, axis=1), weight_ref[first * depth : last * depth, :], preferred_element_type=jnp.float32
    )


def kernel(
    bands, halves, fine_ref, coarse_ref, pos_hbm, wq_hbm, wk_hbm, wv_hbm, wo_hbm, w1_hbm, w2_hbm, lift_hbm, mine,
    other, moved, coarse, x_ref, f_ref, pos_ref, wq_ref, wk_ref, wv_ref, wo_ref, w1_ref, w2_ref, lift_ref,
    edges, part_out, part_in,
    weight_sems, local_sems, fine_send, fine_recv, halo_send, halo_recv, part_send, part_recv,
):
    own, rows, cols, width = mine.shape
    half = rows // 2
    span = cols // CHUNKS
    thin = cols // STEPS
    early = own // 2
    groups = [(0, thin), (thin, 3 * thin), (4 * thin, cols - 4 * thin)]
    slabs = [(row, 1, at, size) for at, size in groups for row in (0, rows - 1)]
    slabs += [(1, rows - 2, chunk * span, span) for chunk in range(CHUNKS)]
    place, core = lax.axis_index("space"), lax.axis_index("tm")
    has_before, has_after = place > 0, place < bands - 1

    def mine_copy(slab):
        row, count, at, size = slabs[slab]
        where = (slice(None), pl.ds(row, count), pl.ds(at, size))
        return pltpu.make_async_copy(fine_ref.at[where], mine.at[where], local_sems.at[slab])

    def fine_copy(shift, slab):
        row, count, at, size = slabs[slab]
        source = mine if count == 1 else fine_ref
        return pltpu.make_async_remote_copy(
            src_ref=source.at[:, pl.ds(row, count), pl.ds(at, size)],
            dst_ref=other.at[pl.ds((shift - 1) * own, own), pl.ds(row, count), pl.ds(at, size)],
            send_sem=fine_send.at[shift - 1, slab],
            recv_sem=fine_recv.at[shift - 1, slab],
            device_id={"tm": lax.rem(core + halves - shift, halves)},
            device_id_type=MESH,
        )

    def to_after(src, dst, send, recv):
        return pltpu.make_async_remote_copy(
            src_ref=src, dst_ref=dst, send_sem=send, recv_sem=recv, device_id={"space": place + 1}, device_id_type=MESH
        )

    def to_before(src, dst, send, recv):
        return pltpu.make_async_remote_copy(
            src_ref=src, dst_ref=dst, send_sem=send, recv_sem=recv, device_id={"space": place - 1}, device_id_type=MESH
        )

    def part_up(frame):
        return to_after(part_out.at[0, frame], part_in.at[0, frame], part_send.at[0, frame], part_recv.at[0, frame])

    def part_down(frame):
        return to_before(part_out.at[1, frame], part_in.at[1, frame], part_send.at[1, frame], part_recv.at[1, frame])

    def halo_up(frames, span_at, piece):
        return to_after(
            moved.at[frames, rows : rows + HALO, span_at], moved.at[frames, 0:HALO, span_at],
            halo_send.at[0, piece], halo_recv.at[0, piece],
        )

    def halo_down(frames, span_at, piece):
        return to_before(
            moved.at[frames, HALO : 2 * HALO, span_at], moved.at[frames, rows + HALO : rows + 2 * HALO, span_at],
            halo_send.at[1, piece], halo_recv.at[1, piece],
        )

    def both(frames, span_at, piece, act_up, act_down):
        pl.when(has_after)(lambda: act_up(halo_up(frames, span_at, piece)))
        pl.when(has_before)(lambda: act_down(halo_down(frames, span_at, piece)))

    def start(copy):
        copy.start()

    def wait_send(copy):
        copy.wait_send()

    def landed(frames, span_at, piece):
        pl.when(has_before)(lambda: halo_up(frames, span_at, piece).wait_recv())
        pl.when(has_after)(lambda: halo_down(frames, span_at, piece).wait_recv())

    barrier = pltpu.get_barrier_semaphore()
    for shift in range(1, halves):
        pl.semaphore_signal(barrier, inc=1, device_id={"tm": lax.rem(core + shift, halves)}, device_id_type=MESH)

    @pl.when(has_before)
    def _():
        pl.semaphore_signal(barrier, inc=1, device_id={"space": place - 1}, device_id_type=MESH)

    @pl.when(has_after)
    def _():
        pl.semaphore_signal(barrier, inc=1, device_id={"space": place + 1}, device_id_type=MESH)

    motion_weights = [
        pltpu.make_async_copy(src, dst, weight_sems.at[at])
        for at, (src, dst) in enumerate(
            [(pos_hbm, pos_ref), (wq_hbm, wq_ref), (wk_hbm, wk_ref), (wv_hbm, wv_ref), (wo_hbm, wo_ref)]
        )
    ]
    later_weights = [
        pltpu.make_async_copy(src, dst, weight_sems.at[5 + at])
        for at, (src, dst) in enumerate(
            [(lift_hbm, lift_ref), (w1_hbm, w1_ref), (w2_hbm, w2_ref), (coarse_ref, coarse)]
        )
    ]
    for slab in range(2):
        mine_copy(slab).start()
    for copy in motion_weights:
        copy.start()
    for slab in range(2, len(slabs)):
        mine_copy(slab).start()
    for copy in later_weights:
        copy.start()

    @pl.when(jnp.logical_not(has_before))
    def _():
        moved[:, 0:HALO] = jnp.zeros((own, HALO, cols, width), jnp.bfloat16)
        part_in[0] = jnp.zeros((own, cols, width), jnp.bfloat16)

    @pl.when(jnp.logical_not(has_after))
    def _():
        moved[:, rows + HALO :] = jnp.zeros((own, HALO, cols, width), jnp.bfloat16)
        part_in[1] = jnp.zeros((own, cols, width), jnp.bfloat16)

    peers = halves - 1 + has_before.astype(jnp.int32) + has_after.astype(jnp.int32)
    pl.semaphore_wait(barrier, peers)

    for slab in range(len(slabs)):
        if slabs[slab][1] == 1:
            mine_copy(slab).wait()
        for shift in range(1, halves):
            fine_copy(shift, slab).start()
    for copy in motion_weights:
        copy.wait()

    pos = []
    for shift in range(halves):
        for frame in range(own):
            pos.append(pos_ref[pl.ds(lax.rem(core + shift, halves) * own + frame, 1), :])

    def motion_tile(places):
        here = [jnp.concatenate([mine[frame, row, at, :] for row, at in places]) for frame in range(own)]
        there = [
            jnp.concatenate([other[frame, row, at, :] for row, at in places]) for frame in range(own * (halves - 1))
        ]
        branch = attention(here, there, pos, wq_ref, wk_ref, wv_ref, wo_ref)
        for frame in range(own):
            result = (here[frame].astype(jnp.float32) + branch[frame]).astype(jnp.bfloat16)
            size = result.shape[0] // len(places)
            for n, (row, at) in enumerate(places):
                moved[frame, row + HALO, at, :] = result[n * size : (n + 1) * size]

    def fine_landed(slab):
        for shift in range(1, halves):
            fine_copy(shift, slab).wait_recv()

    def edge_step(step, carry):
        at = pl.ds(pl.multiple_of(step * thin, thin), thin)
        for group, when in enumerate((0, 1, 4)):

            @pl.when(step == when)
            def _():
                fine_landed(2 * group)
                fine_landed(2 * group + 1)

        motion_tile([(0, at), (rows - 1, at)])

        @pl.when(step == 0)
        def _():
            both(pl.ds(0, own), pl.ds(0, thin), 0, start, start)

        @pl.when(step > 0)
        def _():
            both(pl.ds(0, early), at, step, start, start)

        return carry

    def inner_step(step, carry):
        chunk, row = step // (rows - 2), 1 + lax.rem(step, rows - 2)
        for n in range(CHUNKS):

            @pl.when(step == n * (rows - 2))
            def _():
                mine_copy(2 * len(groups) + n).wait()
                fine_landed(2 * len(groups) + n)

        motion_tile([(row, pl.ds(pl.multiple_of(chunk * span, span), span))])
        return carry

    lax.fori_loop(0, STEPS, edge_step, 0)
    rest = pl.ds(thin, cols - thin)
    for frame in range(early, own):
        both(pl.ds(frame, 1), rest, STEPS + frame - early, start, start)
    lax.fori_loop(0, CHUNKS * (rows - 2), inner_step, 0)

    for copy in later_weights:
        copy.wait()

    def lifted(near, far):
        return jnp.dot(lift_ref[...], jnp.concatenate([near, far], axis=0), preferred_element_type=jnp.float32)

    def first_row(frame, r):
        first = conv_rows(x_ref.at[frame], r, 0, 3, cols, w1_ref)
        first = jnp.maximum(first, 0.0).astype(jnp.bfloat16).astype(jnp.float32)
        spread_columns(f_ref.at[frame], r, first, cols)

    def part_step(frame, carry):
        @pl.when(frame == 0)
        def _():
            landed(pl.ds(0, own), pl.ds(0, thin), 0)
            for step in range(1, STEPS):
                landed(pl.ds(0, early), pl.ds(step * thin, thin), step)

        @pl.when(frame >= early)
        def _():
            landed(pl.ds(frame, 1), rest, STEPS + frame - early)

        for r in range(rows + 2 * HALO):
            spread_columns(x_ref.at[frame], r, jnp.maximum(moved[frame, r].astype(jnp.float32), 0.0), cols)
        none = jnp.zeros_like(coarse[frame, 0])
        first_row(frame, rows - 1)
        part = conv_rows(f_ref.at[frame], rows - 1, 0, 1, cols, w2_ref) + lifted(none, coarse[frame, half - 1])
        part_out[0, frame] = part.astype(jnp.bfloat16)
        first_row(frame, 0)
        part = conv_rows(f_ref.at[frame], -2, 2, 3, cols, w2_ref) + lifted(none, coarse[frame, 0])
        part_out[1, frame] = part.astype(jnp.bfloat16)
        pl.when(has_after)(lambda: part_up(frame).start())
        pl.when(has_before)(lambda: part_down(frame).start())
        return carry

    def conv_step(frame, carry):
        for r in range(1, rows - 1):
            first_row(frame, r)
        for r in range(rows):
            near = coarse[frame, r // 2]
            none = jnp.zeros_like(near)
            if r == 0:
                far = jnp.where(has_before, none, near)
            elif r == rows - 1:
                far = jnp.where(has_after, none, near)
            else:
                far = coarse[frame, r // 2 - 1] if r % 2 == 0 else coarse[frame, r // 2 + 1]
            first_tap, last_tap = 1 if r == 0 else 0, 2 if r == rows - 1 else 3
            second = conv_rows(f_ref.at[frame], r - 1, first_tap, last_tap, cols, w2_ref)
            joined = lifted(near, far) + moved[frame, r + HALO].astype(jnp.float32) + second
            if r == 0:
                edges[frame, 0] = joined
            elif r == rows - 1:
                edges[frame, 1] = joined
            else:
                mine[frame, r] = joined.astype(jnp.bfloat16)
        return carry

    lax.fori_loop(0, own, part_step, 0)
    for shift in range(1, halves):
        for slab in range(len(slabs)):
            fine_copy(shift, slab).wait_send()
    lax.fori_loop(0, own, conv_step, 0)

    def join_step(frame, carry):
        pl.when(has_before)(lambda: part_up(frame).wait_recv())
        mine[frame, 0] = (edges[frame, 0] + part_in[0, frame].astype(jnp.float32)).astype(jnp.bfloat16)
        pl.when(has_after)(lambda: part_down(frame).wait_recv())
        mine[frame, rows - 1] = (edges[frame, 1] + part_in[1, frame].astype(jnp.float32)).astype(jnp.bfloat16)
        return carry

    lax.fori_loop(0, own, join_step, 0)
    for frame in range(own):
        pl.when(has_after)(lambda: part_up(frame).wait_send())
        pl.when(has_before)(lambda: part_down(frame).wait_send())
    both(pl.ds(0, own), pl.ds(0, thin), 0, wait_send, wait_send)
    for step in range(1, STEPS):
        both(pl.ds(0, early), pl.ds(step * thin, thin), step, wait_send, wait_send)
    for frame in range(early, own):
        both(pl.ds(frame, 1), rest, STEPS + frame - early, wait_send, wait_send)


def local(fine, coarse, w_query, w_key, w_value, w_out, conv_first, conv_second):
    own, rows, cols, width = fine.shape
    _, half, small, _ = coarse.shape
    bands, halves = lax.axis_size("space"), lax.axis_size("tm")
    pieces = STEPS + own - own // 2
    far = own * (halves - 1)
    slabs = 6 + CHUNKS
    any_space = pl.BlockSpec(memory_space=pl.ANY)
    bf16 = jnp.bfloat16
    pos = jnp.asarray(encode(own * halves, width))
    lift = jnp.asarray(lift_matrix(small))
    return pl.pallas_call(
        functools.partial(kernel, bands, halves),
        in_specs=[any_space] * 10,
        out_specs=pl.BlockSpec(memory_space=pltpu.VMEM),
        out_shape=pltpu.VMEM(fine.shape, bf16),
        scratch_shapes=[
            pltpu.VMEM((far, rows, cols, width), bf16),
            pltpu.VMEM((own, rows + 2 * HALO, cols, width), bf16),
            pltpu.VMEM((own, half, small, width), bf16),
            pltpu.VMEM((own, (rows + 2 * HALO) * cols, 3 * width), bf16),
            pltpu.VMEM((own, rows * cols, 3 * width), bf16),
            pltpu.VMEM(pos.shape, jnp.float32),
            pltpu.VMEM((width, width), bf16),
            pltpu.VMEM((width, width), bf16),
            pltpu.VMEM((width, width), bf16),
            pltpu.VMEM((width, width), bf16),
            pltpu.VMEM((9 * width, width), bf16),
            pltpu.VMEM((9 * width, width), bf16),
            pltpu.VMEM(lift.shape, bf16),
            pltpu.VMEM((own, 2, cols, width), jnp.float32),
            pltpu.VMEM((2, own, cols, width), bf16),
            pltpu.VMEM((2, own, cols, width), bf16),
            pltpu.SemaphoreType.DMA((9,)),
            pltpu.SemaphoreType.DMA((slabs,)),
            pltpu.SemaphoreType.DMA((halves - 1, slabs)),
            pltpu.SemaphoreType.DMA((halves - 1, slabs)),
            pltpu.SemaphoreType.DMA((2, pieces)),
            pltpu.SemaphoreType.DMA((2, pieces)),
            pltpu.SemaphoreType.DMA((2, own)),
            pltpu.SemaphoreType.DMA((2, own)),
        ],
        compiler_params=pltpu.CompilerParams(
            collective_id=0, has_side_effects=True, vmem_limit_bytes=54 * 1024 * 1024
        ),
        name="fused",
    )(
        fine, coarse, pos, w_query, w_key, w_value, w_out,
        conv_first.reshape(9 * width, width), conv_second.reshape(9 * width, width), lift,
    )


def solution(mesh):
    return jax.shard_map(
        local,
        mesh=mesh,
        in_specs=(
            P("tm", "space", None, None),
            P("tm", "space", None, None),
            P(),
            P(),
            P(),
            P(),
            P(),
            P(),
        ),
        out_specs=P("tm", "space", None, None),
        check_vma=False,
    )
```

time: 60.5 us -> 55.5 us (0.917)
  Pallas kernels: 57.2 us -> 54 us
  local copies, waits for them, and re-layouts: 3.1 us -> 1.32 us
    pallas_call x1, Pallas kernels: 57.2 us -> 54 us  [local(): pl.pallas_call(functools.partial(kernel, bands, halves), in_specs=[any_sp...]
    unnamed x1, local copies, waits for them, and re-layouts: 3.1 us -> 1.32 us
where the time goes in v1:
time: 55.5 us; the launch traced here: 55.4 us
  Pallas kernels  54 us (97%)
  local copies, waits for them, and re-layouts  1.32 us (2%)
    pallas_call x1, Pallas kernels, local(): pl.pallas_call(functools.partial(kernel, bands, halves), in_specs=[any_sp...  54 us
    unnamed x1, local copies, waits for them, and re-layouts  1.32 us

profile of v1, /device:TPU:0, one launch (start us, length us, event | category | flops | bytes accessed | tf_op | source)
XLA Modules:
  0.0 55.4 jit_solution(2332410903819421865)
XLA Ops:
  0.0 54.0 %fused.1 = bf16[4,4,256,256]{3,2,1,0:T(8,128)(2,1)S(1)} custom-call(bf16[4,4,256,256]{3,2,1,0:T(8,128)(2,1)} %fine_ref.1, bf16[4,2,128,256]{3,2,1,0:T(8,128)(2,1)} %coarse_ref.1, f32[8,256]{1,0:T(8,128)} %constant.4.clone.pos_hbm, bf16[256,256]{1,0:T(8,128)(2,1)} %wq_hbm.1, bf16[256,256]{1,0:T(8,128)(2,1)} %wk_hbm.1, bf16[256,256]{1,0:T(8,128)(2,1)} %wv_hbm.1, ...), custom_call_target="tpu_custom_call" | custom-call | tf_op jit(solution)/shard_map/fused/pallas_call | solution.py:370
  54.0 1.3 %copy.12 = bf16[4,4,256,256]{3,2,1,0:T(8,128)(2,1)} copy(bf16[4,4,256,256]{3,2,1,0:T(8,128)(2,1)S(1)} %fused.1) | data formatting | bytes 4194304

commit v2 on v1

v2 whole, which is shorter than its diff:
```python
import functools

import jax
import jax.numpy as jnp
import numpy as np
from jax import lax
from jax.experimental import pallas as pl
from jax.experimental.pallas import tpu as pltpu
from jax.sharding import PartitionSpec as P

HEADS = 8
CHUNKS = 4
STEPS = 8
HALO = 1
LOG2E = 1.4426950408889634
MESH = pl.DeviceIdType.MESH


def encode(frames, width):
    half = width // 2
    inverse = np.exp(-np.log(10000.0) * 2.0 * np.arange(half) / width)
    angles = np.arange(frames)[:, None] * inverse[None, :]
    return np.concatenate([np.sin(angles), np.cos(angles)], axis=1).astype(np.float32)


def lift_matrix(small):
    out = np.arange(2 * small)[:, None]
    source = np.arange(small)[None, :]
    near = out // 2
    far = np.clip(np.where(out % 2 == 0, near - 1, near + 1), 0, small - 1)
    base = 0.75 * (source == near) + 0.25 * (source == far)
    return np.concatenate([0.75 * base, 0.25 * base], axis=1).astype(jnp.bfloat16)


def project(frames, own, pos, wq_ref, wk_ref, wv_ref, query_ref, key_ref, value_ref):
    tile, width = frames[0].shape
    scale = LOG2E / (float(width // HEADS) ** 0.5)
    normed = []
    for x, place in zip(frames, pos):
        hidden = x.astype(jnp.float32) + place
        center = hidden - jnp.mean(hidden, axis=-1, keepdims=True)
        spread = jnp.mean(center * center, axis=-1, keepdims=True)
        normed.append((center * lax.rsqrt(spread + 1e-05)).astype(jnp.bfloat16))
    flat = jnp.concatenate(normed, axis=0)
    query = jnp.dot(flat[: own * tile], wq_ref[...], preferred_element_type=jnp.float32)
    query_ref[...] = (query * scale).astype(jnp.bfloat16)
    key_ref[...] = jnp.dot(flat, wk_ref[...], preferred_element_type=jnp.float32).astype(jnp.bfloat16)
    value_ref[...] = jnp.dot(flat, wv_ref[...], preferred_element_type=jnp.float32).astype(jnp.bfloat16)


def iotas(rows, cols):
    return lax.broadcasted_iota(jnp.int32, (rows, cols), 0), lax.broadcasted_iota(jnp.int32, (rows, cols), 1)


def halve_heads(weight):
    width = weight.shape[1]
    depth = width // HEADS
    half = depth // 2
    source, place = iotas(width, width)
    side, lane = place // (width // 2), lax.rem(place, width // 2)
    wanted = lane // half * depth + side * half + lax.rem(lane, half)
    order = jnp.where(source == wanted, 1.0, 0.0).astype(jnp.bfloat16)
    return jnp.dot(weight, order, preferred_element_type=jnp.float32).astype(jnp.bfloat16)


def mix(tile, query_ref, key_ref, value_ref, wo_ref):
    size, width = query_ref.shape
    own, half = size // tile, width // 2
    query = query_ref[...].reshape(own, tile, width)
    source, place = iotas(2 * width, width)
    same_frame = source // width == place // half
    same_head = lax.rem(source, width) // (width // HEADS) == lax.rem(place, half) // (half // HEADS)
    blocks = jnp.where(same_frame & same_head, 1.0, 0.0).astype(jnp.bfloat16)
    places = [slice(at * tile, (at + 1) * tile) for at in range(key_ref.shape[0] // tile)]
    products = [(query * key_ref[at][None]).reshape(size, width) for at in places]
    scores = []
    for at in range(0, len(places), 2):
        pair = jnp.concatenate(products[at : at + 2], axis=1)
        pair = jnp.dot(pair, blocks, preferred_element_type=jnp.float32)
        scores += [pair[:, :half], pair[:, half:]]
    largest = functools.reduce(jnp.maximum, scores)
    total, summed = None, [None, None]
    for at, score in zip(places, scores):
        power = jnp.exp2(score - largest).reshape(own, tile, half)
        total = power if total is None else total + power
        for side in range(2):
            term = power * value_ref[at, side * half : (side + 1) * half].astype(jnp.float32)[None]
            summed[side] = term if summed[side] is None else summed[side] + term
    inverse = 1.0 / total
    attended = jnp.concatenate([(part * inverse).astype(jnp.bfloat16).reshape(size, half) for part in summed], axis=1)
    branch = jnp.dot(attended, wo_ref[...].reshape(width, width), preferred_element_type=jnp.float32)
    return branch.reshape(own, tile, width)


def spread_columns(ref, at, row, cols):
    column = lax.broadcasted_iota(jnp.int32, row.shape, 0)
    left = jnp.where(column == 0, 0.0, pltpu.roll(row, 1, 0))
    right = jnp.where(column == cols - 1, 0.0, pltpu.roll(row, cols - 1, 0))
    width = row.shape[1]
    ref[at * cols : (at + 1) * cols, :width] = left.astype(jnp.bfloat16)
    ref[at * cols : (at + 1) * cols, width : 2 * width] = row.astype(jnp.bfloat16)
    ref[at * cols : (at + 1) * cols, 2 * width :] = right.astype(jnp.bfloat16)


def conv_rows(ref, start, first, last, cols, weight_ref):
    pieces = [ref[(start + step) * cols : (start + step + 1) * cols, :] for step in range(first, last)]
    depth = ref.shape[1]
    return jnp.dot(
        jnp.concatenate(pieces, axis=1), weight_ref[first * depth : last * depth, :], preferred_element_type=jnp.float32
    )


def kernel(
    bands, halves, fine_ref, coarse_ref, pos_hbm, wq_hbm, wk_hbm, wv_hbm, wo_hbm, w1_hbm, w2_hbm, lift_hbm, mine,
    other, moved, coarse, x_ref, f_ref, pos_ref, wq_ref, wk_ref, wv_ref, wo_ref, w1_ref, w2_ref, lift_ref,
    edges, part_out, part_in, ring, query0, key0, value0, query1, key1, value1,
    weight_sems, local_sems, fine_send, fine_recv, halo_send, halo_recv, part_send, part_recv,
    ring_send, ring_recv, pass_send, pass_recv,
):
    own, rows, cols, width = mine.shape
    half = rows // 2
    span = cols // CHUNKS
    thin = cols // STEPS
    early = own // 2
    pieces = 2 * STEPS - 2
    groups = [(0, thin), (thin, thin), (2 * thin, 2 * thin), (4 * thin, cols - 4 * thin)]
    slabs = [(row, 1, at, size) for at, size in groups for row in (0, rows - 1)]
    slabs += [(1, rows - 2, chunk * span, span) for chunk in range(CHUNKS)]
    slots = ((query0, key0, value0), (query1, key1, value1))
    place, core = lax.axis_index("space"), lax.axis_index("tm")
    has_before, has_after = place > 0, place < bands - 1
    near_after = lax.rem(place, 2) == 0
    near_before = jnp.logical_not(near_after)

    def mine_copy(slab):
        row, count, at, size = slabs[slab]
        where = (slice(None), pl.ds(row, count), pl.ds(at, size))
        return pltpu.make_async_copy(fine_ref.at[where], mine.at[where], local_sems.at[slab])

    def fine_copy(shift, slab):
        row, count, at, size = slabs[slab]
        source = mine if count == 1 else fine_ref
        return pltpu.make_async_remote_copy(
            src_ref=source.at[:, pl.ds(row, count), pl.ds(at, size)],
            dst_ref=other.at[pl.ds((shift - 1) * own, own), pl.ds(row, count), pl.ds(at, size)],
            send_sem=fine_send.at[shift - 1, slab],
            recv_sem=fine_recv.at[shift - 1, slab],
            device_id={"tm": lax.rem(core + halves - shift, halves)},
            device_id_type=MESH,
        )

    def to_after(src, dst, send, recv):
        return pltpu.make_async_remote_copy(
            src_ref=src, dst_ref=dst, send_sem=send, recv_sem=recv, device_id={"space": place + 1}, device_id_type=MESH
        )

    def to_before(src, dst, send, recv):
        return pltpu.make_async_remote_copy(
            src_ref=src, dst_ref=dst, send_sem=send, recv_sem=recv, device_id={"space": place - 1}, device_id_type=MESH
        )

    def part_up(frame):
        return to_after(part_out.at[0, frame], part_in.at[0, frame], part_send.at[0, frame], part_recv.at[0, frame])

    def part_down(frame):
        return to_before(part_out.at[1, frame], part_in.at[1, frame], part_send.at[1, frame], part_recv.at[1, frame])

    def ring_up():
        return to_after(mine.at[:, rows - 1, 0:thin], ring.at[0, 0:own], ring_send.at[0], ring_recv.at[0])

    def ring_down():
        return to_before(mine.at[:, 0, 0:thin], ring.at[1, 0:own], ring_send.at[1], ring_recv.at[1])

    def ring_pass(shift):
        return pltpu.make_async_remote_copy(
            src_ref=ring.at[:, 0:own],
            dst_ref=ring.at[:, pl.ds(shift * own, own)],
            send_sem=pass_send.at[shift - 1],
            recv_sem=pass_recv.at[shift - 1],
            device_id={"tm": lax.rem(core + halves - shift, halves)},
            device_id_type=MESH,
        )

    def halo_up(frames, span_at, piece):
        return to_after(
            moved.at[frames, rows : rows + HALO, span_at], moved.at[frames, 0:HALO, span_at],
            halo_send.at[0, piece], halo_recv.at[0, piece],
        )

    def halo_down(frames, span_at, piece):
        return to_before(
            moved.at[frames, HALO : 2 * HALO, span_at], moved.at[frames, rows + HALO : rows + 2 * HALO, span_at],
            halo_send.at[1, piece], halo_recv.at[1, piece],
        )

    def start(copy):
        copy.start()

    def wait_send(copy):
        copy.wait_send()

    def piece(at, act, up_if, down_if):
        for first, low, high in ((0, 0, early), (STEPS - 1, early, own)):

            @pl.when((at >= first) & (at < first + STEPS - 1))
            def _():
                columns = pl.ds(pl.multiple_of((at - first + 1) * thin, thin), thin)
                frames = pl.ds(low, high - low)
                pl.when(up_if)(lambda: act(halo_up(frames, columns, at)))
                pl.when(down_if)(lambda: act(halo_down(frames, columns, at)))

    def each_piece(low, high, act, up_if, down_if):
        lax.fori_loop(low, high, lambda at, carry: (piece(at, act, up_if, down_if), carry)[1], 0)

    def wait_recv(copy):
        copy.wait_recv()

    def landed(low, high):
        each_piece(low, high, wait_recv, has_before, has_after)

    barrier = pltpu.get_barrier_semaphore()
    for shift in range(1, halves):
        pl.semaphore_signal(barrier, inc=1, device_id={"tm": lax.rem(core + shift, halves)}, device_id_type=MESH)

    @pl.when(has_before)
    def _():
        pl.semaphore_signal(barrier, inc=1, device_id={"space": place - 1}, device_id_type=MESH)

    @pl.when(has_after)
    def _():
        pl.semaphore_signal(barrier, inc=1, device_id={"space": place + 1}, device_id_type=MESH)

    motion_weights = [
        pltpu.make_async_copy(src, dst, weight_sems.at[at])
        for at, (src, dst) in enumerate(
            [(wv_hbm, wv_ref), (pos_hbm, pos_ref), (wq_hbm, wq_ref), (wk_hbm, wk_ref)]
            + [(wo_hbm.at[:, side], wo_ref.at[side]) for side in range(2)]
        )
    ]
    later_weights = [
        pltpu.make_async_copy(src, dst, weight_sems.at[6 + at])
        for at, (src, dst) in enumerate(
            [(lift_hbm, lift_ref), (w1_hbm, w1_ref), (w2_hbm, w2_ref), (coarse_ref, coarse)]
        )
    ]
    for slab in range(4):
        mine_copy(slab).start()
    for copy in motion_weights:
        copy.start()
    for slab in range(4, len(slabs)):
        mine_copy(slab).start()
    for copy in later_weights:
        copy.start()

    @pl.when(jnp.logical_not(has_before))
    def _():
        moved[:, 0:HALO] = jnp.zeros((own, HALO, cols, width), jnp.bfloat16)
        part_in[0] = jnp.zeros((own, cols, width), jnp.bfloat16)
        ring[0, 0:own] = jnp.zeros((own, thin, width), jnp.bfloat16)

    @pl.when(jnp.logical_not(has_after))
    def _():
        moved[:, rows + HALO :] = jnp.zeros((own, HALO, cols, width), jnp.bfloat16)
        part_in[1] = jnp.zeros((own, cols, width), jnp.bfloat16)
        ring[1, 0:own] = jnp.zeros((own, thin, width), jnp.bfloat16)

    motion_weights[0].wait()
    wv_ref[...] = halve_heads(wv_ref[...])
    peers = halves - 1 + has_before.astype(jnp.int32) + has_after.astype(jnp.int32)
    pl.semaphore_wait(barrier, peers)

    mine_copy(0).wait()
    mine_copy(1).wait()
    pl.when(has_after)(lambda: ring_up().start())
    pl.when(has_before)(lambda: ring_down().start())
    for slab in (2, 3, 4, 5, 6, 7, 0, 1, *range(8, len(slabs))):
        if 2 <= slab < 8:
            mine_copy(slab).wait()
        for shift in range(1, halves):
            fine_copy(shift, slab).start()
    for copy in motion_weights[1:]:
        copy.wait()

    pos = []
    for shift in range(halves):
        for frame in range(own):
            pos.append(pos_ref[pl.ds(lax.rem(core + shift, halves) * own + frame, 1), :])

    def fine_landed(slab):
        for shift in range(1, halves):
            fine_copy(shift, slab).wait_recv()

    needs = {0: (2, 3), 1: (4, 5), 3: (6, 7), STEPS - 1: (0, 1)}
    for chunk in range(CHUNKS):
        needs[STEPS + max(chunk * STEPS // CHUNKS - 1, 0)] = (2 * len(groups) + chunk,)

    def places_of(tile):
        pair, step = tile // STEPS, lax.rem(tile + 1, STEPS)
        at = pl.ds(pl.multiple_of(step * thin, thin), thin)
        return (pair, at), (rows - 1 - pair, at)

    def arrive(tile):
        for when, waits in needs.items():

            @pl.when(tile == when)
            def _():
                for slab in waits:
                    if slabs[slab][1] > 1:
                        mine_copy(slab).wait()
                    fine_landed(slab)

        pl.when(tile == STEPS - 2)(pass_ring)

    def pass_ring():
        pl.when(has_before)(lambda: ring_up().wait_recv())
        pl.when(has_after)(lambda: ring_down().wait_recv())
        for shift in range(1, halves):
            ring_pass(shift).start()

    def enter_ring(slot):
        frames = [jnp.concatenate([ring[0, frame], ring[1, frame]]) for frame in range(own * halves)]
        project(frames, own, pos, wq_ref, wk_ref, wv_ref, *slots[slot])

    def leave_ring(slot):
        branch = mix(2 * thin, *slots[slot], wo_ref)
        for frame in range(own):
            for side, real in enumerate((has_before, has_after)):
                result = ring[side, frame].astype(jnp.float32) + branch[frame, side * thin : (side + 1) * thin]
                moved[frame, side * (rows + HALO), 0:thin, :] = jnp.where(real, result, 0.0).astype(jnp.bfloat16)

    def enter(tile, slot):
        places = places_of(tile)
        frames = [jnp.concatenate([mine[frame, row, at, :] for row, at in places]) for frame in range(own)]
        frames += [
            jnp.concatenate([other[frame, row, at, :] for row, at in places]) for frame in range(own * (halves - 1))
        ]
        project(frames, own, pos, wq_ref, wk_ref, wv_ref, *slots[slot])

    def leave(tile, slot):
        places = places_of(tile)
        branch = mix(2 * thin, *slots[slot], wo_ref)
        for frame in range(own):
            for n, (row, at) in enumerate(places):
                result = mine[frame, row, at, :].astype(jnp.float32) + branch[frame, n * thin : (n + 1) * thin]
                moved[frame, row + HALO, at, :] = result.astype(jnp.bfloat16)

    def hand_over(tile):
        now = tile < STEPS - 1
        piece(tile, start, has_after & (now | near_after), has_before & (now | near_before))

    def turn(tile, slot):
        arrive(tile + 1)
        leave(tile, slot)
        enter(tile + 1, 1 - slot)
        hand_over(tile)

    def two_turns(step, carry):
        turn(2 * step, 0)
        turn(2 * step + 1, 1)
        return carry

    tiles = STEPS * (rows // 2)
    arrive(0)
    enter(0, 0)
    lax.fori_loop(0, tiles // 2 - 1, two_turns, 0)
    turn(tiles - 2, 0)
    for shift in range(1, halves):
        ring_pass(shift).wait_recv()
    leave(tiles - 1, 1)
    enter_ring(0)
    each_piece(STEPS - 1, pieces, start, has_after & near_before, has_before & near_after)
    each_piece(tiles - 1, pieces, start, has_after & near_after, has_before & near_before)
    leave_ring(0)

    for copy in later_weights:
        copy.wait()

    def lifted(near, far):
        return jnp.dot(lift_ref[...], jnp.concatenate([near, far], axis=0), preferred_element_type=jnp.float32)

    def first_row(frame, r):
        first = conv_rows(x_ref.at[frame], r, 0, 3, cols, w1_ref)
        first = jnp.maximum(first, 0.0).astype(jnp.bfloat16).astype(jnp.float32)
        spread_columns(f_ref.at[frame], r, first, cols)

    def part_step(frame):
        pl.when(frame == 0)(lambda: landed(0, STEPS - 1))
        for r in range(rows + 2 * HALO):
            spread_columns(x_ref.at[frame], r, jnp.maximum(moved[frame, r].astype(jnp.float32), 0.0), cols)
        none = jnp.zeros_like(coarse[frame, 0])
        first_row(frame, rows - 1)
        part = conv_rows(f_ref.at[frame], rows - 1, 0, 1, cols, w2_ref) + lifted(none, coarse[frame, half - 1])
        part_out[0, frame] = part.astype(jnp.bfloat16)
        first_row(frame, 0)
        part = conv_rows(f_ref.at[frame], -2, 2, 3, cols, w2_ref) + lifted(none, coarse[frame, 0])
        part_out[1, frame] = part.astype(jnp.bfloat16)
        now = frame > 1
        pl.when(has_after & (now | near_after))(lambda: part_up(frame).start())
        pl.when(has_before & (now | near_before))(lambda: part_down(frame).start())

    def held_parts():
        landed(STEPS - 1, pieces)
        for frame in range(2):
            pl.when(has_after & near_before)(lambda: part_up(frame).start())
            pl.when(has_before & near_after)(lambda: part_down(frame).start())

    def conv_step(frame):
        for r in range(1, rows - 1):
            first_row(frame, r)
        for r in range(rows):
            near = coarse[frame, r // 2]
            none = jnp.zeros_like(near)
            if r == 0:
                far = jnp.where(has_before, none, near)
            elif r == rows - 1:
                far = jnp.where(has_after, none, near)
            else:
                far = coarse[frame, r // 2 - 1] if r % 2 == 0 else coarse[frame, r // 2 + 1]
            first_tap, last_tap = 1 if r == 0 else 0, 2 if r == rows - 1 else 3
            second = conv_rows(f_ref.at[frame], r - 1, first_tap, last_tap, cols, w2_ref)
            joined = lifted(near, far) + moved[frame, r + HALO].astype(jnp.float32) + second
            if r == 0:
                edges[frame, 0] = joined
            elif r == rows - 1:
                edges[frame, 1] = joined
            else:
                mine[frame, r] = joined.astype(jnp.bfloat16)

    def conv_turn(turn, carry):
        pl.when(turn >= 2)(lambda: conv_step(turn - 2))
        pl.when(turn == 2)(held_parts)
        pl.when(turn < own)(lambda: part_step(turn))
        return carry

    for shift in range(1, halves):
        for slab in range(len(slabs)):
            fine_copy(shift, slab).wait_send()
    lax.fori_loop(0, own + 2, conv_turn, 0)

    each_piece(0, pieces, wait_send, has_after, has_before)
    pl.when(has_after)(lambda: ring_up().wait_send())
    pl.when(has_before)(lambda: ring_down().wait_send())
    for shift in range(1, halves):
        ring_pass(shift).wait_send()

    def join_step(frame, carry):
        pl.when(has_after)(lambda: part_up(frame).wait_send())
        pl.when(has_before)(lambda: part_down(frame).wait_send())
        pl.when(has_before)(lambda: part_up(frame).wait_recv())
        mine[frame, 0] = (edges[frame, 0] + part_in[0, frame].astype(jnp.float32)).astype(jnp.bfloat16)
        pl.when(has_after)(lambda: part_down(frame).wait_recv())
        mine[frame, rows - 1] = (edges[frame, 1] + part_in[1, frame].astype(jnp.float32)).astype(jnp.bfloat16)
        return carry

    lax.fori_loop(0, own, join_step, 0)


def local(fine, coarse, w_query, w_key, w_value, w_out, conv_first, conv_second):
    own, rows, cols, width = fine.shape
    _, half, small, _ = coarse.shape
    bands, halves = lax.axis_size("space"), lax.axis_size("tm")
    pieces = 2 * STEPS - 2
    far = own * (halves - 1)
    slabs = 8 + CHUNKS
    halved = (2, HEADS, width // HEADS // 2, width)
    any_space = pl.BlockSpec(memory_space=pl.ANY)
    bf16 = jnp.bfloat16
    pos = jnp.asarray(encode(own * halves, width))
    lift = jnp.asarray(lift_matrix(small))
    return pl.pallas_call(
        functools.partial(kernel, bands, halves),
        in_specs=[any_space] * 10,
        out_specs=pl.BlockSpec(memory_space=pltpu.VMEM),
        out_shape=pltpu.VMEM(fine.shape, bf16),
        scratch_shapes=[
            pltpu.VMEM((far, rows, cols, width), bf16),
            pltpu.VMEM((own, rows + 2 * HALO, cols, width), bf16),
            pltpu.VMEM((own, half, small, width), bf16),
            pltpu.VMEM((own, (rows + 2 * HALO) * cols, 3 * width), bf16),
            pltpu.VMEM((own, rows * cols, 3 * width), bf16),
            pltpu.VMEM(pos.shape, jnp.float32),
            pltpu.VMEM((width, width), bf16),
            pltpu.VMEM((width, width), bf16),
            pltpu.VMEM((width, width), bf16),
            pltpu.VMEM(halved, bf16),
            pltpu.VMEM((9 * width, width), bf16),
            pltpu.VMEM((9 * width, width), bf16),
            pltpu.VMEM(lift.shape, bf16),
            pltpu.VMEM((own, 2, cols, width), jnp.float32),
            pltpu.VMEM((2, own, cols, width), bf16),
            pltpu.VMEM((2, own, cols, width), bf16),
            pltpu.VMEM((2, own * halves, cols // STEPS, width), bf16),
            *[pltpu.VMEM((count * 2 * cols // STEPS, width), bf16) for count in (own, own + far, own + far)] * 2,
            pltpu.SemaphoreType.DMA((10,)),
            pltpu.SemaphoreType.DMA((slabs,)),
            pltpu.SemaphoreType.DMA((halves - 1, slabs)),
            pltpu.SemaphoreType.DMA((halves - 1, slabs)),
            pltpu.SemaphoreType.DMA((2, pieces)),
            pltpu.SemaphoreType.DMA((2, pieces)),
            pltpu.SemaphoreType.DMA((2, own)),
            pltpu.SemaphoreType.DMA((2, own)),
            pltpu.SemaphoreType.DMA((2,)),
            pltpu.SemaphoreType.DMA((2,)),
            pltpu.SemaphoreType.DMA((halves - 1,)),
            pltpu.SemaphoreType.DMA((halves - 1,)),
        ],
        compiler_params=pltpu.CompilerParams(
            collective_id=0, has_side_effects=True, vmem_limit_bytes=54 * 1024 * 1024
        ),
        name="fused",
    )(
        fine, coarse, pos, w_query, w_key, w_value,
        w_out.reshape(HEADS, 2, width // HEADS // 2, width), conv_first.reshape(9 * width, width), conv_second.reshape(9 * width, width), lift,
    )


def solution(mesh):
    return jax.shard_map(
        local,
        mesh=mesh,
        in_specs=(
            P("tm", "space", None, None),
            P("tm", "space", None, None),
            P(),
            P(),
            P(),
            P(),
            P(),
            P(),
        ),
        out_specs=P("tm", "space", None, None),
        check_vma=False,
    )
```

time: 55.5 us -> 53.7 us (0.968)
  Pallas kernels: 54 us -> 52.2 us
    pallas_call x1, Pallas kernels: 54 us -> 52.2 us  [local(): pl.pallas_call(functools.partial(kernel, bands, halves), in_specs=[any_sp...]
where the time goes in v2:
time: 53.7 us; the launch traced here: 53.6 us
  Pallas kernels  52.2 us (97%)
  local copies, waits for them, and re-layouts  1.32 us (2%)
    pallas_call x1, Pallas kernels, local(): pl.pallas_call(functools.partial(kernel, bands, halves), in_specs=[any_sp...  52.2 us
    unnamed x1, local copies, waits for them, and re-layouts  1.32 us

profile of v2, /device:TPU:0, one launch (start us, length us, event | category | flops | bytes accessed | tf_op | source)
XLA Modules:
  0.0 53.6 jit_solution(17325237792811595549)
XLA Ops:
  0.0 52.2 %fused.1 = bf16[4,4,256,256]{3,2,1,0:T(8,128)(2,1)S(1)} custom-call(bf16[4,4,256,256]{3,2,1,0:T(8,128)(2,1)} %fine_ref.1, bf16[4,2,128,256]{3,2,1,0:T(8,128)(2,1)} %coarse_ref.1, f32[8,256]{1,0:T(8,128)} %constant.4.clone.pos_hbm, bf16[256,256]{1,0:T(8,128)(2,1)} %wq_hbm.1, bf16[256,256]{1,0:T(8,128)(2,1)} %wk_hbm.1, bf16[256,256]{1,0:T(8,128)(2,1)} %wv_hbm.1, ...), custom_call_target="tpu_custom_call" | custom-call | tf_op jit(solution)/shard_map/fused/pallas_call | solution.py:470
  52.2 1.3 %copy.12 = bf16[4,4,256,256]{3,2,1,0:T(8,128)(2,1)} copy(bf16[4,4,256,256]{3,2,1,0:T(8,128)(2,1)S(1)} %fused.1) | data formatting | bytes 4194304

commit v3 on v2

--- a/solution.py
+++ b/solution.py
@@ -126,6 +126,7 @@
     groups = [(0, thin), (thin, thin), (2 * thin, 2 * thin), (4 * thin, cols - 4 * thin)]
     slabs = [(row, 1, at, size) for at, size in groups for row in (0, rows - 1)]
     slabs += [(1, rows - 2, chunk * span, span) for chunk in range(CHUNKS)]
+    lots = [slab // 2 if slab < 2 * len(groups) else slab - len(groups) for slab in range(len(slabs))]
     slots = ((query0, key0, value0), (query1, key1, value1))
     place, core = lax.axis_index("space"), lax.axis_index("tm")
     has_before, has_after = place > 0, place < bands - 1
@@ -135,7 +136,7 @@
     def mine_copy(slab):
         row, count, at, size = slabs[slab]
         where = (slice(None), pl.ds(row, count), pl.ds(at, size))
-        return pltpu.make_async_copy(fine_ref.at[where], mine.at[where], local_sems.at[slab])
+        return pltpu.make_async_copy(fine_ref.at[where], mine.at[where], local_sems.at[lots[slab]])
 
     def fine_copy(shift, slab):
         row, count, at, size = slabs[slab]
@@ -143,11 +144,44 @@
         return pltpu.make_async_remote_copy(
             src_ref=source.at[:, pl.ds(row, count), pl.ds(at, size)],
             dst_ref=other.at[pl.ds((shift - 1) * own, own), pl.ds(row, count), pl.ds(at, size)],
-            send_sem=fine_send.at[shift - 1, slab],
-            recv_sem=fine_recv.at[shift - 1, slab],
+            send_sem=fine_send.at[shift - 1],
+            recv_sem=fine_recv.at[shift - 1, lots[slab]],
             device_id={"tm": lax.rem(core + halves - shift, halves)},
             device_id_type=MESH,
         )
+
+    def lot_part(lot):
+        if lot < len(groups):
+            return (slice(None), pl.ds(0, 2), pl.ds(*groups[lot]))
+        row, count, at, size = slabs[lot + len(groups)]
+        return (slice(None), pl.ds(row, count), pl.ds(at, size))
+
+    def mine_landed(lot):
+        where = lot_part(lot)
+        pltpu.make_async_copy(fine_ref.at[where], mine.at[where], local_sems.at[lot]).wait()
+
+    def fine_landed(lot):
+        where = lot_part(lot)
+        for shift in range(1, halves):
+            pltpu.make_async_remote_copy(
+                src_ref=mine.at[where],
+                dst_ref=other.at[pl.ds((shift - 1) * own, own), *where[1:]],
+                send_sem=fine_send.at[shift - 1],
+                recv_sem=fine_recv.at[shift - 1, lot],
+                device_id={"tm": lax.rem(core + halves - shift, halves)},
+                device_id_type=MESH,
+            ).wait_recv()
+
+    def fine_left():
+        for shift in range(1, halves):
+            pltpu.make_async_remote_copy(
+                src_ref=mine,
+                dst_ref=other.at[pl.ds((shift - 1) * own, own)],
+                send_sem=fine_send.at[shift - 1],
+                recv_sem=fine_recv.at[shift - 1, 0],
+                device_id={"tm": lax.rem(core + halves - shift, halves)},
+                device_id_type=MESH,
+            ).wait_send()
 
     def to_after(src, dst, send, recv):
         return pltpu.make_async_remote_copy(
@@ -160,10 +194,10 @@
         )
 
     def part_up(frame):
-        return to_after(part_out.at[0, frame], part_in.at[0, frame], part_send.at[0, frame], part_recv.at[0, frame])
+        return to_after(part_out.at[0, frame], part_in.at[0, frame], part_send.at[0], part_recv.at[0, frame])
 
     def part_down(frame):
-        return to_before(part_out.at[1, frame], part_in.at[1, frame], part_send.at[1, frame], part_recv.at[1, frame])
+        return to_before(part_out.at[1, frame], part_in.at[1, frame], part_send.at[1], part_recv.at[1, frame])
 
     def ring_up():
         return to_after(mine.at[:, rows - 1, 0:thin], ring.at[0, 0:own], ring_send.at[0], ring_recv.at[0])
@@ -181,43 +215,39 @@
             device_id_type=MESH,
         )
 
-    def halo_up(frames, span_at, piece):
+    def halo_up(frames, span_at, late):
         return to_after(
             moved.at[frames, rows : rows + HALO, span_at], moved.at[frames, 0:HALO, span_at],
-            halo_send.at[0, piece], halo_recv.at[0, piece],
-        )
-
-    def halo_down(frames, span_at, piece):
+            halo_send.at[0], halo_recv.at[0, late],
+        )
+
+    def halo_down(frames, span_at, late):
         return to_before(
             moved.at[frames, HALO : 2 * HALO, span_at], moved.at[frames, rows + HALO : rows + 2 * HALO, span_at],
-            halo_send.at[1, piece], halo_recv.at[1, piece],
-        )
-
-    def start(copy):
-        copy.start()
-
-    def wait_send(copy):
-        copy.wait_send()
-
-    def piece(at, act, up_if, down_if):
-        for first, low, high in ((0, 0, early), (STEPS - 1, early, own)):
-
-            @pl.when((at >= first) & (at < first + STEPS - 1))
+            halo_send.at[1], halo_recv.at[1, late],
+        )
+
+    crowd = ((0, early), (early, own - early), (0, own))
+
+    def piece(at, up_if, down_if):
+        for late in range(2):
+
+            @pl.when((at >= late * (STEPS - 1)) & (at < (late + 1) * (STEPS - 1)))
             def _():
-                columns = pl.ds(pl.multiple_of((at - first + 1) * thin, thin), thin)
-                frames = pl.ds(low, high - low)
-                pl.when(up_if)(lambda: act(halo_up(frames, columns, at)))
-                pl.when(down_if)(lambda: act(halo_down(frames, columns, at)))
-
-    def each_piece(low, high, act, up_if, down_if):
-        lax.fori_loop(low, high, lambda at, carry: (piece(at, act, up_if, down_if), carry)[1], 0)
-
-    def wait_recv(copy):
-        copy.wait_recv()
-
-    def landed(low, high):
-        each_piece(low, high, wait_recv, has_before, has_after)
-
+                columns = pl.ds(pl.multiple_of((at - late * (STEPS - 1) + 1) * thin, thin), thin)
+                frames = pl.ds(*crowd[late])
+                pl.when(up_if)(lambda: halo_up(frames, columns, late).start())
+                pl.when(down_if)(lambda: halo_down(frames, columns, late).start())
+
+    def each_piece(low, high, up_if, down_if):
+        lax.fori_loop(low, high, lambda at, carry: (piece(at, up_if, down_if), carry)[1], 0)
+
+    def landed(late):
+        frames = pl.ds(*crowd[late])
+        pl.when(has_before)(lambda: halo_up(frames, rest, late).wait_recv())
+        pl.when(has_after)(lambda: halo_down(frames, rest, late).wait_recv())
+
+    rest = pl.ds(thin, cols - thin)
     barrier = pltpu.get_barrier_semaphore()
     for shift in range(1, halves):
         pl.semaphore_signal(barrier, inc=1, device_id={"tm": lax.rem(core + shift, halves)}, device_id_type=MESH)
@@ -264,20 +294,19 @@
         part_in[1] = jnp.zeros((own, cols, width), jnp.bfloat16)
         ring[1, 0:own] = jnp.zeros((own, thin, width), jnp.bfloat16)
 
-    motion_weights[0].wait()
-    wv_ref[...] = halve_heads(wv_ref[...])
     peers = halves - 1 + has_before.astype(jnp.int32) + has_after.astype(jnp.int32)
     pl.semaphore_wait(barrier, peers)
 
-    mine_copy(0).wait()
-    mine_copy(1).wait()
+    mine_landed(0)
     pl.when(has_after)(lambda: ring_up().start())
     pl.when(has_before)(lambda: ring_down().start())
     for slab in (2, 3, 4, 5, 6, 7, 0, 1, *range(8, len(slabs))):
-        if 2 <= slab < 8:
-            mine_copy(slab).wait()
+        if slab in (2, 4, 6):
+            mine_landed(lots[slab])
         for shift in range(1, halves):
             fine_copy(shift, slab).start()
+    motion_weights[0].wait()
+    wv_ref[...] = halve_heads(wv_ref[...])
     for copy in motion_weights[1:]:
         copy.wait()
 
@@ -286,13 +315,9 @@
         for frame in range(own):
             pos.append(pos_ref[pl.ds(lax.rem(core + shift, halves) * own + frame, 1), :])
 
-    def fine_landed(slab):
-        for shift in range(1, halves):
-            fine_copy(shift, slab).wait_recv()
-
-    needs = {0: (2, 3), 1: (4, 5), 3: (6, 7), STEPS - 1: (0, 1)}
+    needs = {0: 1, 1: 2, 3: 3, STEPS - 1: 0}
     for chunk in range(CHUNKS):
-        needs[STEPS + max(chunk * STEPS // CHUNKS - 1, 0)] = (2 * len(groups) + chunk,)
+        needs[STEPS + max(chunk * STEPS // CHUNKS - 1, 0)] = len(groups) + chunk
 
     def places_of(tile):
         pair, step = tile // STEPS, lax.rem(tile + 1, STEPS)
@@ -300,14 +325,13 @@
         return (pair, at), (rows - 1 - pair, at)
 
     def arrive(tile):
-        for when, waits in needs.items():
+        for when, lot in needs.items():
 
             @pl.when(tile == when)
             def _():
-                for slab in waits:
-                    if slabs[slab][1] > 1:
-                        mine_copy(slab).wait()
-                    fine_landed(slab)
+                if lot >= len(groups):
+                    mine_landed(lot)
+                fine_landed(lot)
 
         pl.when(tile == STEPS - 2)(pass_ring)
 
@@ -346,7 +370,11 @@
 
     def hand_over(tile):
         now = tile < STEPS - 1
-        piece(tile, start, has_after & (now | near_after), has_before & (now | near_before))
+        piece(tile, has_after & (now | near_after), has_before & (now | near_before))
+
+        @pl.when(tile == 12)
+        def _():
+            each_piece(STEPS - 1, pieces, has_after & near_before, has_before & near_after)
 
     def turn(tile, slot):
         arrive(tile + 1)
@@ -368,8 +396,7 @@
         ring_pass(shift).wait_recv()
     leave(tiles - 1, 1)
     enter_ring(0)
-    each_piece(STEPS - 1, pieces, start, has_after & near_before, has_before & near_after)
-    each_piece(tiles - 1, pieces, start, has_after & near_after, has_before & near_before)
+    each_piece(tiles - 1, pieces, has_after & near_after, has_before & near_before)
     leave_ring(0)
 
     for copy in later_weights:
@@ -384,7 +411,7 @@
         spread_columns(f_ref.at[frame], r, first, cols)
 
     def part_step(frame):
-        pl.when(frame == 0)(lambda: landed(0, STEPS - 1))
+        pl.when(frame == 0)(lambda: landed(0))
         for r in range(rows + 2 * HALO):
             spread_columns(x_ref.at[frame], r, jnp.maximum(moved[frame, r].astype(jnp.float32), 0.0), cols)
         none = jnp.zeros_like(coarse[frame, 0])
@@ -399,7 +426,7 @@
         pl.when(has_before & (now | near_before))(lambda: part_down(frame).start())
 
     def held_parts():
-        landed(STEPS - 1, pieces)
+        landed(1)
         for frame in range(2):
             pl.when(has_after & near_before)(lambda: part_up(frame).start())
             pl.when(has_before & near_after)(lambda: part_down(frame).start())
@@ -432,20 +459,17 @@
         pl.when(turn < own)(lambda: part_step(turn))
         return carry
 
-    for shift in range(1, halves):
-        for slab in range(len(slabs)):
-            fine_copy(shift, slab).wait_send()
+    fine_left()
     lax.fori_loop(0, own + 2, conv_turn, 0)
 
-    each_piece(0, pieces, wait_send, has_after, has_before)
+    pl.when(has_after)(lambda: halo_up(pl.ds(*crowd[2]), rest, 0).wait_send())
+    pl.when(has_before)(lambda: halo_down(pl.ds(*crowd[2]), rest, 0).wait_send())
     pl.when(has_after)(lambda: ring_up().wait_send())
     pl.when(has_before)(lambda: ring_down().wait_send())
     for shift in range(1, halves):
         ring_pass(shift).wait_send()
 
     def join_step(frame, carry):
-        pl.when(has_after)(lambda: part_up(frame).wait_send())
-        pl.when(has_before)(lambda: part_down(frame).wait_send())
         pl.when(has_before)(lambda: part_up(frame).wait_recv())
         mine[frame, 0] = (edges[frame, 0] + part_in[0, frame].astype(jnp.float32)).astype(jnp.bfloat16)
         pl.when(has_after)(lambda: part_down(frame).wait_recv())
@@ -453,15 +477,16 @@
         return carry
 
     lax.fori_loop(0, own, join_step, 0)
+    pl.when(has_after)(lambda: to_after(part_out.at[0], part_in.at[0], part_send.at[0], part_recv.at[0, 0]).wait_send())
+    pl.when(has_before)(lambda: to_before(part_out.at[1], part_in.at[1], part_send.at[1], part_recv.at[1, 0]).wait_send())
 
 
 def local(fine, coarse, w_query, w_key, w_value, w_out, conv_first, conv_second):
     own, rows, cols, width = fine.shape
     _, half, small, _ = coarse.shape
     bands, halves = lax.axis_size("space"), lax.axis_size("tm")
-    pieces = 2 * STEPS - 2
     far = own * (halves - 1)
-    slabs = 8 + CHUNKS
+    lots = 4 + CHUNKS
     halved = (2, HEADS, width // HEADS // 2, width)
     any_space = pl.BlockSpec(memory_space=pl.ANY)
     bf16 = jnp.bfloat16
@@ -492,12 +517,12 @@
             pltpu.VMEM((2, own * halves, cols // STEPS, width), bf16),
             *[pltpu.VMEM((count * 2 * cols // STEPS, width), bf16) for count in (own, own + far, own + far)] * 2,
             pltpu.SemaphoreType.DMA((10,)),
-            pltpu.SemaphoreType.DMA((slabs,)),
-            pltpu.SemaphoreType.DMA((halves - 1, slabs)),
-            pltpu.SemaphoreType.DMA((halves - 1, slabs)),
-            pltpu.SemaphoreType.DMA((2, pieces)),
-            pltpu.SemaphoreType.DMA((2, pieces)),
-            pltpu.SemaphoreType.DMA((2, own)),
+            pltpu.SemaphoreType.DMA((lots,)),
+            pltpu.SemaphoreType.DMA((halves - 1,)),
+            pltpu.SemaphoreType.DMA((halves - 1, lots)),
+            pltpu.SemaphoreType.DMA((2,)),
+            pltpu.SemaphoreType.DMA((2, 2)),
+            pltpu.SemaphoreType.DMA((2,)),
             pltpu.SemaphoreType.DMA((2, own)),
             pltpu.SemaphoreType.DMA((2,)),
             pltpu.SemaphoreType.DMA((2,)),

time: 53.7 us -> 51.8 us (0.965)
  Pallas kernels: 52.2 us -> 50.4 us
    pallas_call x1, Pallas kernels: 52.2 us -> 50.4 us  [local(): pl.pallas_call(functools.partial(kernel, bands, halves), in_specs=[any_sp...]
where the time goes in v3:
time: 51.8 us; the launch traced here: 51.7 us
  Pallas kernels  50.4 us (97%)
  local copies, waits for them, and re-layouts  1.32 us (3%)
    pallas_call x1, Pallas kernels, local(): pl.pallas_call(functools.partial(kernel, bands, halves), in_specs=[any_sp...  50.4 us
    unnamed x1, local copies, waits for them, and re-layouts  1.32 us

profile of v3, /device:TPU:0, one launch (start us, length us, event | category | flops | bytes accessed | tf_op | source)
XLA Modules:
  0.0 51.7 jit_solution(13987142591367920300)
XLA Ops:
  0.0 50.4 %fused.1 = bf16[4,4,256,256]{3,2,1,0:T(8,128)(2,1)S(1)} custom-call(bf16[4,4,256,256]{3,2,1,0:T(8,128)(2,1)} %fine_ref.1, bf16[4,2,128,256]{3,2,1,0:T(8,128)(2,1)} %coarse_ref.1, f32[8,256]{1,0:T(8,128)} %constant.4.clone.pos_hbm, bf16[256,256]{1,0:T(8,128)(2,1)} %wq_hbm.1, bf16[256,256]{1,0:T(8,128)(2,1)} %wk_hbm.1, bf16[256,256]{1,0:T(8,128)(2,1)} %wv_hbm.1, ...), custom_call_target="tpu_custom_call" | custom-call | tf_op jit(solution)/shard_map/fused/pallas_call | solution.py:495
  50.4 1.3 %copy.12 = bf16[4,4,256,256]{3,2,1,0:T(8,128)(2,1)} copy(bf16[4,4,256,256]{3,2,1,0:T(8,128)(2,1)S(1)} %fused.1) | data formatting | bytes 4194304

commit v4 on v3

--- a/solution.py
+++ b/solution.py
@@ -229,19 +229,6 @@
 
     crowd = ((0, early), (early, own - early), (0, own))
 
-    def piece(at, up_if, down_if):
-        for late in range(2):
-
-            @pl.when((at >= late * (STEPS - 1)) & (at < (late + 1) * (STEPS - 1)))
-            def _():
-                columns = pl.ds(pl.multiple_of((at - late * (STEPS - 1) + 1) * thin, thin), thin)
-                frames = pl.ds(*crowd[late])
-                pl.when(up_if)(lambda: halo_up(frames, columns, late).start())
-                pl.when(down_if)(lambda: halo_down(frames, columns, late).start())
-
-    def each_piece(low, high, up_if, down_if):
-        lax.fori_loop(low, high, lambda at, carry: (piece(at, up_if, down_if), carry)[1], 0)
-
     def landed(late):
         frames = pl.ds(*crowd[late])
         pl.when(has_before)(lambda: halo_up(frames, rest, late).wait_recv())
@@ -370,11 +357,14 @@
 
     def hand_over(tile):
         now = tile < STEPS - 1
-        piece(tile, has_after & (now | near_after), has_before & (now | near_before))
-
-        @pl.when(tile == 12)
-        def _():
-            each_piece(STEPS - 1, pieces, has_after & near_before, has_before & near_after)
+        columns = pl.ds(pl.multiple_of((tile + 1) * thin, thin), thin)
+        pl.when(has_after & now)(lambda: halo_up(pl.ds(*crowd[0]), columns, 0).start())
+        pl.when(has_before & now)(lambda: halo_down(pl.ds(*crowd[0]), columns, 0).start())
+        local, transit = tile == STEPS - 1, tile == 12
+        up_if = has_after & ((near_after & local) | (near_before & transit))
+        down_if = has_before & ((near_before & local) | (near_after & transit))
+        pl.when(up_if)(lambda: halo_up(pl.ds(*crowd[1]), rest, 1).start())
+        pl.when(down_if)(lambda: halo_down(pl.ds(*crowd[1]), rest, 1).start())
 
     def turn(tile, slot):
         arrive(tile + 1)
@@ -396,7 +386,6 @@
         ring_pass(shift).wait_recv()
     leave(tiles - 1, 1)
     enter_ring(0)
-    each_piece(tiles - 1, pieces, has_after & near_after, has_before & near_before)
     leave_ring(0)
 
     for copy in later_weights:
@@ -421,9 +410,12 @@
         first_row(frame, 0)
         part = conv_rows(f_ref.at[frame], -2, 2, 3, cols, w2_ref) + lifted(none, coarse[frame, 0])
         part_out[1, frame] = part.astype(jnp.bfloat16)
-        now = frame > 1
-        pl.when(has_after & (now | near_after))(lambda: part_up(frame).start())
-        pl.when(has_before & (now | near_before))(lambda: part_down(frame).start())
+        pl.when(has_after & near_after)(lambda: part_up(frame).start())
+        pl.when(has_before & near_before)(lambda: part_down(frame).start())
+
+    def far_part(frame):
+        pl.when(has_after & near_before)(lambda: part_up(frame).start())
+        pl.when(has_before & near_after)(lambda: part_down(frame).start())
 
     def held_parts():
         landed(1)
@@ -457,6 +449,7 @@
         pl.when(turn >= 2)(lambda: conv_step(turn - 2))
         pl.when(turn == 2)(held_parts)
         pl.when(turn < own)(lambda: part_step(turn))
+        pl.when(turn > 3)(lambda: far_part(turn - 2))
         return carry
 
     fine_left()

time: 51.8 us -> 51.1 us (0.986)
  Pallas kernels: 50.4 us -> 49.2 us
    pallas_call x1, Pallas kernels: 50.4 us -> 49.2 us  [local(): pl.pallas_call(functools.partial(kernel, bands, halves), in_specs=[any_sp...]
where the time goes in v4:
time: 51.1 us; the launch traced here: 50.5 us
  Pallas kernels  49.2 us (96%)
  local copies, waits for them, and re-layouts  1.32 us (3%)
    pallas_call x1, Pallas kernels, local(): pl.pallas_call(functools.partial(kernel, bands, halves), in_specs=[any_sp...  49.2 us
    unnamed x1, local copies, waits for them, and re-layouts  1.32 us

profile of v4, /device:TPU:0, one launch (start us, length us, event | category | flops | bytes accessed | tf_op | source)
XLA Modules:
  0.0 50.5 jit_solution(16482574608965200524)
XLA Ops:
  0.0 49.2 %fused.1 = bf16[4,4,256,256]{3,2,1,0:T(8,128)(2,1)S(1)} custom-call(bf16[4,4,256,256]{3,2,1,0:T(8,128)(2,1)} %fine_ref.1, bf16[4,2,128,256]{3,2,1,0:T(8,128)(2,1)} %coarse_ref.1, f32[8,256]{1,0:T(8,128)} %constant.4.clone.pos_hbm, bf16[256,256]{1,0:T(8,128)(2,1)} %wq_hbm.1, bf16[256,256]{1,0:T(8,128)(2,1)} %wk_hbm.1, bf16[256,256]{1,0:T(8,128)(2,1)} %wv_hbm.1, ...), custom_call_target="tpu_custom_call" | custom-call | tf_op jit(solution)/shard_map/fused/pallas_call | solution.py:488
  49.2 1.3 %copy.12 = bf16[4,4,256,256]{3,2,1,0:T(8,128)(2,1)} copy(bf16[4,4,256,256]{3,2,1,0:T(8,128)(2,1)S(1)} %fused.1) | data formatting | bytes 4194304

commit v5 on v4

--- a/solution.py
+++ b/solution.py
@@ -9,7 +9,7 @@
 from jax.sharding import PartitionSpec as P
 
 HEADS = 8
-CHUNKS = 4
+CHUNKS = 2
 STEPS = 8
 HALO = 1
 LOG2E = 1.4426950408889634
@@ -281,6 +281,8 @@
         part_in[1] = jnp.zeros((own, cols, width), jnp.bfloat16)
         ring[1, 0:own] = jnp.zeros((own, thin, width), jnp.bfloat16)
 
+    motion_weights[0].wait()
+    wv_ref[...] = halve_heads(wv_ref[...])
     peers = halves - 1 + has_before.astype(jnp.int32) + has_after.astype(jnp.int32)
     pl.semaphore_wait(barrier, peers)
 
@@ -292,8 +294,6 @@
             mine_landed(lots[slab])
         for shift in range(1, halves):
             fine_copy(shift, slab).start()
-    motion_weights[0].wait()
-    wv_ref[...] = halve_heads(wv_ref[...])
     for copy in motion_weights[1:]:
         copy.wait()
 

time: 51.1 us -> 51.1 us (level)
  no operation moved by 1% of the time
where the time goes in v5:
time: 51.1 us; the launch traced here: 50.5 us
  Pallas kernels  49.1 us (96%)
  local copies, waits for them, and re-layouts  1.32 us (3%)
    pallas_call x1, Pallas kernels, local(): pl.pallas_call(functools.partial(kernel, bands, halves), in_specs=[any_sp...  49.1 us
    unnamed x1, local copies, waits for them, and re-layouts  1.32 us

profile of v5, /device:TPU:0, one launch (start us, length us, event | category | flops | bytes accessed | tf_op | source)
XLA Modules:
  0.0 50.5 jit_solution(5217975828029724683)
XLA Ops:
  0.0 49.1 %fused.1 = bf16[4,4,256,256]{3,2,1,0:T(8,128)(2,1)S(1)} custom-call(bf16[4,4,256,256]{3,2,1,0:T(8,128)(2,1)} %fine_ref.1, bf16[4,2,128,256]{3,2,1,0:T(8,128)(2,1)} %coarse_ref.1, f32[8,256]{1,0:T(8,128)} %constant.4.clone.pos_hbm, bf16[256,256]{1,0:T(8,128)(2,1)} %wq_hbm.1, bf16[256,256]{1,0:T(8,128)(2,1)} %wk_hbm.1, bf16[256,256]{1,0:T(8,128)(2,1)} %wv_hbm.1, ...), custom_call_target="tpu_custom_call" | custom-call | tf_op jit(solution)/shard_map/fused/pallas_call | solution.py:488
  49.1 1.3 %copy.12 = bf16[4,4,256,256]{3,2,1,0:T(8,128)(2,1)} copy(bf16[4,4,256,256]{3,2,1,0:T(8,128)(2,1)S(1)} %fused.1) | data formatting | bytes 4194304
